TPU v7x, 32 devices: a whole 2x2x4 slice. The times are simulated.
32 devices in a mesh: expert: 8 (over y, x, core), tensor: 4 (over z).
Axes of the slice: x: 2, y: 2, z: 4, core: 2. Of those that a mesh axis runs over, the one named last changes fastest.
Arguments:
- tokens: bfloat16 [1024, 2560], P('expert', 'tensor'), may hold values from -6 to 6
- slot: int32 [1024, 1], P('expert'), may hold values from 0 to 15; in each aligned block of 128 rows (0 to 127, 128 to 255, ...) at most 16 rows name the same one
- mask: int32 [1024], P('expert'), may hold values 0 or 1
- hot_group: int32 [1], replicated, may hold values from 0 to 7
- router_weight: bfloat16 [2560, 8], replicated, may hold values from -0.125 to 0.125
- exp_gate: bfloat16 [8, 2560, 4096], P('expert', None, 'tensor'), may hold values from -0.125 to 0.125
- exp_up: bfloat16 [8, 2560, 4096], P('expert', None, 'tensor'), may hold values from -0.125 to 0.125
- exp_down: bfloat16 [8, 4096, 2560], P('expert', 'tensor'), may hold values from -0.09375 to 0.09375
- sh_gate: bfloat16 [2560, 4096], P('expert', 'tensor'), may hold values from -0.125 to 0.125
- sh_up: bfloat16 [2560, 4096], P('expert', 'tensor'), may hold values from -0.125 to 0.125
- sh_down: bfloat16 [4096, 2560], P('tensor', 'expert'), may hold values from -0.09375 to 0.09375
Outputs:
- mixed: bfloat16 [1024, 2560], P('expert', 'tensor')
Inputs may be any that keep to these rules, and one draw needn't show every extreme that they name: Slot 2 g is the home slot of expert g, slot 2 g + 1 the spare slot of group g. Among the 128 tokens of one group no slot is named by more than 16 tokens, a bound that some block reaches.
All inputs are finite; a program needn't handle non-finite values. No bound on the sum of `mask` on one device may be relied on, other than what follows from the above.
Results may differ from a plain program's by a relative error of at most 0.0052.
Values may be sent and summed in bfloat16 or wider, within the bound.
No kernel may reach another device: no remote copies, remote signals or barrier semaphores. Data moves between devices by JAX's collectives and lax.ppermute only.
A program may use at most 192 MiB of HBM per device.

v0:
```python
import functools

import jax
import jax.numpy as jnp
from jax import lax
from jax.experimental import pallas as pl
from jax.experimental.pallas import tpu as pltpu
from jax.sharding import PartitionSpec as P


F32, BF16 = jnp.float32, jnp.bfloat16
ROWS = 512
BLOCK = 512
ANY, VMEM = pl.BlockSpec(memory_space=pl.ANY), pl.BlockSpec(memory_space=pltpu.VMEM)
HBM, SMEM = pl.BlockSpec(memory_space=pltpu.HBM), pl.BlockSpec(memory_space=pltpu.SMEM)
DMA = pltpu.SemaphoreType.DMA
MIB = 1024 * 1024


def swap(block, axis, bit):
    return lax.ppermute(block, axis, [(i, i ^ bit) for i in range(lax.axis_size(axis))])


def tie(*values):
    return lax.optimization_barrier(values)


def orders(size):
    bits = [1 << k for k in range(1, size.bit_length() - 1)]
    turn = len(bits) // 2
    return bits, bits[turn:] + bits[:turn]


def silu(v):
    return v / (1.0 + jnp.exp(-v))


def cost(flops, bytes_accessed):
    return pl.CostEstimate(flops=flops, bytes_accessed=bytes_accessed, transcendentals=0)


def stage_kernel(*refs):
    n = len(refs) // 2
    sources, targets, sems = refs[:n], refs[n : 2 * n], refs[2 * n]
    copies = [pltpu.make_async_copy(s, t, sems.at[i]) for i, (s, t) in enumerate(zip(sources, targets))]
    for copy in copies:
        copy.start()
    for copy in copies:
        copy.wait()


def stage(weights):
    return pl.pallas_call(
        stage_kernel,
        out_shape=tuple(pltpu.VMEM(w.shape, BF16) for w in weights),
        in_specs=[HBM] * len(weights),
        out_specs=(VMEM,) * len(weights),
        scratch_shapes=[DMA((len(weights),))],
        compiler_params=pltpu.CompilerParams(vmem_limit_bytes=42 * MIB),
        cost_estimate=cost(5 * 10**9, 2 * sum(w.size for w in weights)),
        name="stage",
    )(*weights)


def hidden_kernel(n_pieces, meta, *refs):
    pieces, (router, gate, up, hidden, x, sem) = refs[:n_pieces], refs[n_pieces:]
    width, units = gate.shape[1:]
    span = pieces[0].shape[0]
    loads = [pltpu.make_async_copy(p, x.at[pl.ds(i * span, span), :], sem.at[i]) for i, p in enumerate(pieces)]
    for copy in loads:
        copy.start()
    for copy in loads:
        copy.wait()
    batch = x[:, :width]
    slots = x[:, width : width + 1].astype(F32)
    home = jnp.floor(slots * 0.5)
    chosen = jnp.where(slots == 2.0 * home, home, meta[1].astype(F32)) == meta[0].astype(F32)
    logits = lax.dot_general(batch, router[...], (((1,), (1,)), ((), ())), preferred_element_type=F32)
    column = lax.broadcasted_iota(jnp.int32, logits.shape, 1) == meta[0]
    logit = jnp.sum(jnp.where(column, logits, 0.0), axis=1, keepdims=True)
    weighting = jnp.where(chosen, 1.0 / (1.0 + jnp.exp(-logit)), 0.0)
    block = min(BLOCK, units)
    for at in range(0, units, block):
        lanes = slice(at, at + block)
        gated = jnp.dot(batch, gate[0, :, lanes], preferred_element_type=F32)
        upward = jnp.dot(batch, up[0, :, lanes], preferred_element_type=F32)
        hidden[:, lanes] = (silu(gated) * upward * weighting).astype(BF16)


def routed_hidden(meta, pieces, weights):
    n_pieces = len(pieces)
    rows, across = n_pieces * pieces[0].shape[0], pieces[0].shape[1]
    width, units = weights[1].shape[1:]
    return pl.pallas_call(
        functools.partial(hidden_kernel, n_pieces),
        out_shape=(pltpu.VMEM((rows, units), BF16), pltpu.VMEM((rows, across), BF16)),
        in_specs=[SMEM] + [ANY] * n_pieces + [VMEM] * 3,
        out_specs=(VMEM, VMEM),
        scratch_shapes=[DMA((n_pieces,))],
        compiler_params=pltpu.CompilerParams(vmem_limit_bytes=10 * MIB),
        cost_estimate=cost(4 * rows * width * units, 4 * width * units),
        name="routed_hidden",
    )(meta, *pieces, *weights[:3])


def down_kernel(n_strips, n_cuts, meta, x, hidden, down, *refs):
    if n_strips:
        strips, refs = refs[:n_strips], refs[n_strips:]
        *outs, p_s, turned, sem = refs
    else:
        p_s, turned, *outs = refs
    width = down.shape[2]
    depth = width // n_cuts
    cols = turned.shape[1]
    places = [pl.ds(pl.multiple_of(meta[2 + k], 128), depth) for k in range(n_cuts)]
    if n_strips:
        strip = strips[0].shape[0]
        rows_of = [pl.ds(pl.multiple_of(meta[2 + n_cuts + j], 16), strip) for j in range(n_strips)]
        loads = [pltpu.make_async_copy(s, p_s.at[rows_of[j], :], sem.at[j]) for j, s in enumerate(strips)]
        for copy in loads:
            copy.start()
        for copy in loads:
            copy.wait()
    both = jnp.dot(x[:, :width], p_s[:, : 2 * cols], preferred_element_type=F32)
    shared = (silu(both[:, :cols]) * both[:, cols:]).astype(BF16)
    n_kept = x.shape[0] // 2
    for k in range(n_cuts):
        if n_strips:
            turned[k] = jnp.transpose(p_s[places[k], 2 * cols :], (1, 0))
        total = jnp.dot(hidden[...], down[0, :, places[k]], preferred_element_type=F32)
        total = total + jnp.dot(shared, turned[k], preferred_element_type=F32)
        kept, sent = outs[2 * (2 * k // n_cuts) : 2 * (2 * k // n_cuts) + 2]
        at = (k % (n_cuts // 2)) * depth
        kept[:, at : at + depth] = total[:n_kept]
        sent[:, at : at + depth] = total[n_kept:].astype(BF16)


def both_down(meta, x, hidden, down, strips, ready, n_cuts):
    rows, width = x.shape[0], down.shape[2]
    if ready:
        cols = ready[1].shape[1]
        extra, more, scratch = list(ready), [], []
    else:
        cols = strips[0].shape[1] // 3
        extra, scratch = list(strips), [DMA((len(strips),))]
        more = [pltpu.VMEM((width, 3 * cols), BF16), pltpu.VMEM((n_cuts, cols, width // n_cuts), BF16)]
    outs = [pltpu.VMEM((rows // 2, width // 2), F32), pltpu.VMEM((rows // 2, width // 2), BF16)] * 2 + more
    units = hidden.shape[1]
    out = pl.pallas_call(
        functools.partial(down_kernel, 0 if ready else len(strips), n_cuts),
        out_shape=tuple(outs),
        in_specs=[SMEM, VMEM, VMEM, VMEM] + [VMEM if ready else ANY] * len(extra),
        out_specs=(VMEM,) * len(outs),
        scratch_shapes=scratch,
        compiler_params=pltpu.CompilerParams(vmem_limit_bytes=8 * MIB),
        cost_estimate=cost(2 * rows * width * (units + 6 * cols), 2 * width * (units + 3 * cols)),
        name="both_down",
    )(meta, x, hidden, down, *extra)
    return [out[0:2], out[2:4]], ready or out[4:6]


def local(
    tokens,
    slot,
    mask,
    hot_group,
    router_weight,
    exp_gate,
    exp_up,
    exp_down,
    sh_gate,
    sh_up,
    sh_down,
):
    n_groups, n_cuts = lax.axis_size("expert"), lax.axis_size("tensor")
    me, cut = lax.axis_index("expert"), lax.axis_index("tensor")
    rows, depth = tokens.shape
    half = rows // 2
    strip, cols = sh_gate.shape[0], sh_gate.shape[1] // n_groups
    relative = list(reversed(range(n_cuts)))
    numbers = [me, hot_group[0]] + [(cut ^ k) * depth for k in relative] + [(me ^ j) * strip for j in range(n_groups)]
    meta = jnp.stack(numbers).astype(jnp.int32)

    features = [tokens] + [swap(tokens, "tensor", k) for k in range(1, n_cuts)]
    names = jnp.broadcast_to(slot.astype(BF16), (rows, 128))
    real = mask.astype(F32)[:, None]

    packed = jnp.concatenate(
        [
            sh_gate.reshape(strip, n_groups, cols).transpose(1, 0, 2),
            sh_up.reshape(strip, n_groups, cols).transpose(1, 0, 2),
            sh_down.reshape(n_groups, cols, strip).transpose(0, 2, 1),
        ],
        axis=2,
    )
    blocks = [lax.dynamic_index_in_dim(packed, me ^ j, 0, keepdims=False) for j in range(n_groups)]
    near_first = sorted(range(1, n_groups), key=lambda j: (j.bit_count(), j))
    soon, rest = near_first[: n_groups // 2 - 1], near_first[n_groups // 2 - 1 :]
    strips = {0: blocks[0]}
    strips.update({j: swap(blocks[j], "expert", j) for j in soon})

    features, names, real, meta, _ = tie(features, names, real, meta, blocks)
    whole = jnp.concatenate([jnp.zeros((rows, depth * n_cuts), BF16), names], axis=1)
    for k, feature in enumerate(features):
        whole = lax.dynamic_update_slice(whole, feature, (0, (cut ^ k) * depth))
    halves = [whole[:half], whole[half:]]
    weights = stage((router_weight.T, exp_gate, exp_up, exp_down))

    routes = orders(n_groups)
    last = len(routes[0]) - 1
    pieces = [{0: piece} for piece in halves]
    mates = [{1: swap(piece, "expert", 1)} for piece in halves]
    early = late = None
    for phase in range(last + 1):
        if phase == last:
            early = [{**p, **m} for p, m in zip(pieces, mates)]
        arrived = [
            {j | r[phase]: swap(b, "expert", r[phase]) for j, b in p.items() if j or phase < last}
            for r, p in zip(routes, pieces)
        ]
        if phase == last:
            arrived = [{r[phase]: swap(p[0], "expert", r[phase]), **new} for r, p, new in zip(routes, pieces, arrived)]
        for p, m, new in zip(pieces, mates, arrived):
            p.update(new)
            m.update({j | 1: swap(b, "expert", 1) for j, b in new.items()})
        if phase == last:
            late = [{**new, **{j | 1: m[j | 1] for j in new}} for m, new in zip(mates, arrived)]
    middle = len(rest) // 2
    for some in (rest[:middle], rest[middle:]):
        strips.update({j: swap(blocks[j], "expert", j) for j in some})
    strips = [strips[j] for j in range(n_groups)]

    def batches(parts):
        even = [(h, j) for h in (0, 1) for j in sorted(parts[h]) if j & 1 == 0]
        many = min(len(even), ROWS // (2 * half))
        for at in range(0, len(even), many):
            stay = even[at : at + many]
            yield stay, [parts[h][j] for h, j in stay] + [parts[h][j | 1] for h, j in stay]

    first, second, ready = [], [], None
    for stay, batch in batches(early):
        first.append((stay, routed_hidden(meta, batch, weights)))
    meta, _ = tie(meta, [done[0] for _, done in first])
    for stay, batch in batches(late):
        second.append((stay, routed_hidden(meta, batch, weights)))

    acc = [[{}, {}], [{}, {}]]

    def settle(stay, parts):
        for c, (kept, sent) in enumerate(parts):
            total = kept + swap(sent, "expert", 1).astype(F32)
            for i, (h, j) in enumerate(stay):
                acc[c][h][j] = total[i * half : (i + 1) * half]

    for stay, (hidden, x) in second:
        parts, ready = both_down(meta, x, hidden, weights[3], strips, ready, n_cuts)
        settle(stay, parts)
    for stay, (hidden, x) in first:
        parts, _ = both_down(meta, x, hidden, weights[3], strips, ready, n_cuts)
        settle(stay, parts)

    for phase in reversed(range(last + 1)):
        for c in (0, 1):
            away = [[j for j in a if j & r[phase]] for r, a in zip(routes, acc[c])]
            sends = [jnp.concatenate([a.pop(j) for j in js], axis=0).astype(BF16) for a, js in zip(acc[c], away)]
            came = tie(*[swap(send, "expert", r[phase]) for r, send in zip(routes, tie(*sends))])
            for r, a, js, got in zip(routes, acc[c], away, came):
                for i, j in enumerate(js):
                    a[j ^ r[phase]] = a[j ^ r[phase]] + got[i * half : (i + 1) * half].astype(F32)
    mixed = None
    for c in (0, 1):
        mine = jnp.concatenate([a[0] for a in acc[c]], axis=0)
        for i, k in enumerate(relative[c * n_cuts // 2 : (c + 1) * n_cuts // 2]):
            part = mine[:, i * depth : (i + 1) * depth]
            if k:
                part = swap(part.astype(BF16), "tensor", k).astype(F32)
            mixed = part if mixed is None else mixed + part
    return (mixed * real).astype(BF16)


def solution(mesh):
    in_specs = (
        P("expert", "tensor"),
        P("expert", None),
        P("expert"),
        P(),
        P(),
        P("expert", None, "tensor"),
        P("expert", None, "tensor"),
        P("expert", "tensor", None),
        P("expert", "tensor"),
        P("expert", "tensor"),
        P("tensor", "expert"),
    )
    out_specs = P("expert", "tensor")
    return jax.shard_map(local, mesh=mesh, in_specs=in_specs, out_specs=out_specs, check_vma=False)
```

profile of v0, /device:TPU:0, one launch (start us, length us, event | category | flops | bytes accessed | tf_op | source)
XLA Modules:
  0.0 126.4 jit_solution(3399891240220904038)
XLA Ops:
  0.0 4.1 %collective-permute-start.1 = (bf16[128,640]{1,0:T(8,128)(2,1)}, bf16[128,640]{1,0:T(8,128)(2,1)S(1)}, u32[]{:S(2)}, u32[]{:S(2)}) collective-permute-start(bf16[128,640]{1,0:T(8,128)(2,1)} %param.11), channel_id=1, source_target_pairs={{0,2},{1,3},{2,0},{3,1},{4,6},{5,7},{6,4},{7,5},{8,10},{9,11},{10,... | collective-permute-start | bytes 491528 | tf_op jit(solution)/shard_map/ppermute | solution.py:21
  4.1 1.6 %collective-permute-start = (bf16[128,640]{1,0:T(8,128)(2,1)}, bf16[128,640]{1,0:T(8,128)(2,1)}, u32[]{:S(2)}, u32[]{:S(2)}) collective-permute-start(bf16[128,640]{1,0:T(8,128)(2,1)} %param.11), channel_id=1, source_target_pairs={{0,1},{1,0},{2,3},{3,2},{4,5},{5,4},{6,7},{7,6},{8,9},{9,8},{10,11... | collective-permute-start | bytes 491528 | tf_op jit(solution)/shard_map/ppermute | solution.py:21
  10.0 3.7 %collective-permute-done.1 = bf16[128,640]{1,0:T(8,128)(2,1)S(1)} collective-permute-done((bf16[128,640]{1,0:T(8,128)(2,1)}, bf16[128,640]{1,0:T(8,128)(2,1)S(1)}, u32[]{:S(2)}, u32[]{:S(2)}) %collective-permute-start.1) | collective-permute-done | bytes 163872 | tf_op jit(solution)/shard_map/ppermute | solution.py:21
  13.7 3.0 %collective-permute-done.2 = bf16[128,640]{1,0:T(8,128)(2,1)S(1)} collective-permute-done((bf16[128,640]{1,0:T(8,128)(2,1)}, bf16[128,640]{1,0:T(8,128)(2,1)S(1)}, u32[]{:S(2)}, u32[]{:S(2)}) %collective-permute-start.2) | collective-permute-done | bytes 163872 | tf_op jit(solution)/shard_map/ppermute | solution.py:21
  18.0 1.6 %collective-permute-start.11 = (bf16[64,2688]{1,0:T(8,128)(2,1)S(1)}, bf16[64,2688]{1,0:T(8,128)(2,1)S(1)}, u32[]{:S(2)}, u32[]{:S(2)}) collective-permute-start(bf16[64,2688]{1,0:T(8,128)(2,1)S(1)} %get-tuple-element.105.refs_2_), channel_id=1, source_target_pairs={{0,8},{4,12},{8,0},{12,4},{16,24},{20,28},{24,16},{28,20},{1,9},{5... | collective-permute-start | bytes 1032200 | tf_op jit(solution)/shard_map/ppermute | solution.py:21
  22.1 6.9 %collective-permute-done.11.refs_2_ = bf16[64,2688]{1,0:T(8,128)(2,1)S(1)} collective-permute-done((bf16[64,2688]{1,0:T(8,128)(2,1)S(1)}, bf16[64,2688]{1,0:T(8,128)(2,1)S(1)}, u32[]{:S(2)}, u32[]{:S(2)}) %collective-permute-start.11) | collective-permute-done | bytes 344096 | tf_op jit(solution)/shard_map/ppermute | solution.py:21
  31.0 5.3 %collective-permute-done.3.refs_1_ = bf16[64,2688]{1,0:T(8,128)(2,1)S(1)} collective-permute-done((bf16[64,2688]{1,0:T(8,128)(2,1)S(1)}, bf16[64,2688]{1,0:T(8,128)(2,1)S(1)}, u32[]{:S(2)}, u32[]{:S(2)}) %collective-permute-start.3) | collective-permute-done | bytes 344096 | tf_op jit(solution)/shard_map/ppermute | solution.py:21
  37.9 5.6 %stage.1 = (bf16[8,2560]{1,0:T(8,128)(2,1)S(1)}, bf16[1,2560,1024]{2,1,0:T(8,128)(2,1)S(1)}, bf16[1,2560,1024]{2,1,0:T(8,128)(2,1)S(1)}, bf16[1,1024,2560]{2,1,0:T(8,128)(2,1)S(1)}) custom-call(bf16[8,2560]{1,0:T(8,128)(2,1)} %bitcast.57, bf16[1,2560,1024]{2,1,0:T(8,128)(2,1)} %refs_1_.1, bf16[1,2560,1024]{2,1,0:T(8,128)(2,1)} %refs_2_.1, ...), custom_call_target="tpu_custom_call" | custom-call | flops 5000000000 | bytes 15769600 | tf_op jit(solution)/shard_map/stage/pallas_call | solution.py:53
  46.0 8.2 %routed_hidden.2 = (bf16[512,1024]{1,0:T(8,128)(2,1)S(1)}, bf16[512,2688]{1,0:T(8,128)(2,1)S(1)}) custom-call(s32[14]{0:T(128)S(1)} %stack.55.meta, bf16[64,2688]{1,0:T(8,128)(2,1)S(1)} %get-tuple-element.106.refs_0_, bf16[64,2688]{1,0:T(8,128)(2,1)S(1)} %collective-permute-done.3.refs_1_, bf16[64,2688]{1,0:T(8,128)(2,1)S(1)} %get-tuple-element.105.refs_2_, ...), custom_call_target="tpu_custom_call" | custom-call | flops 5368709120 | bytes 10485760 | tf_op jit(solution)/shard_map/routed_hidden/pallas_call | solution.py:94
  58.1 8.2 %routed_hidden.3 = (bf16[512,1024]{1,0:T(8,128)(2,1)S(1)}, bf16[512,2688]{1,0:T(8,128)(2,1)S(1)}) custom-call(s32[14]{0:T(128)S(1)} %stack.55.meta, bf16[64,2688]{1,0:T(8,128)(2,1)S(1)} %collective-permute-done.9.refs_0_, bf16[64,2688]{1,0:T(8,128)(2,1)S(1)} %collective-permute-done.10.refs_1_, bf16[64,2688]{1,0:T(8,128)(2,1)S(1)} %collective-permute-done.11.refs_2_, ...), custom_call_target="tpu_custom_call" | custom-call | flops 5368709120 | bytes 10485760 | tf_op jit(solution)/shard_map/routed_hidden/pallas_call | solution.py:94
  66.3 1.6 %collective-permute-done.20.refs_4_ = bf16[320,384]{1,0:T(8,128)(2,1)S(1)} collective-permute-done((bf16[320,384]{1,0:T(8,128)(2,1)S(1)}, bf16[320,384]{1,0:T(8,128)(2,1)S(1)}, u32[]{:S(2)}, u32[]{:S(2)}) %collective-permute-start.20) | collective-permute-done | bytes 245792 | tf_op jit(solution)/shard_map/ppermute | solution.py:21
  67.9 1.9 %collective-permute-done.18.refs_2_ = bf16[320,384]{1,0:T(8,128)(2,1)S(1)} collective-permute-done((bf16[320,384]{1,0:T(8,128)(2,1)S(1)}, bf16[320,384]{1,0:T(8,128)(2,1)S(1)}, u32[]{:S(2)}, u32[]{:S(2)}) %collective-permute-start.18) | collective-permute-done | bytes 245792 | tf_op jit(solution)/shard_map/ppermute | solution.py:21
  69.7 9.1 %both_down.2 = (f32[256,1280]{1,0:T(8,128)S(1)}, bf16[256,1280]{1,0:T(8,128)(2,1)S(1)}, f32[256,1280]{1,0:T(8,128)S(1)}, bf16[256,1280]{1,0:T(8,128)(2,1)S(1)}, ...) custom-call(s32[14]{0:T(128)S(1)} %stack.55.meta, bf16[512,2688]{1,0:T(8,128)(2,1)S(1)} %get-tuple-element.60.x, ...), custom_call_target="tpu_custom_call" | custom-call | flops 4697620480 | bytes 7208960 | tf_op jit(solution)/shard_map/both_down/pallas_call | solution.py:149
  78.9 6.2 %both_down.3 = (f32[256,1280]{1,0:T(8,128)S(1)}, bf16[256,1280]{1,0:T(8,128)(2,1)S(1)}, f32[256,1280]{1,0:T(8,128)S(1)}, bf16[256,1280]{1,0:T(8,128)(2,1)S(1)}) custom-call(s32[14]{0:T(128)S(1)} %stack.55.meta, bf16[512,2688]{1,0:T(8,128)(2,1)S(1)} %get-tuple-element.58.x, bf16[512,1024]{1,0:T(8,128)(2,1)S(1)} %get-tuple-element.56.hidden, ...), custom_call_target="tpu_custom_call" | custom-call | flops 4697620480 | bytes 7208960 | tf_op jit(solution)/shard_map/both_down/pallas_call | solution.py:149
  86.4 1.6 %collective-permute-start.26 = (bf16[128,1280]{1,0:T(8,128)(2,1)S(1)}, bf16[128,1280]{1,0:T(8,128)(2,1)S(1)}, u32[]{:S(2)}, u32[]{:S(2)}) collective-permute-start(bf16[128,1280]{1,0:T(8,128)(2,1)S(1)} %get-tuple-element.68), channel_id=1, source_target_pairs={{0,16},{4,20},{8,24},{12,28},{16,0},{20,4},{24,8},{28,12},{1,17},{... | collective-permute-start | bytes 983048 | tf_op jit(solution)/shard_map/ppermute | solution.py:21
  89.5 1.6 %collective-permute-start.34 = (bf16[128,1280]{1,0:T(8,128)(2,1)S(1)}, bf16[128,1280]{1,0:T(8,128)(2,1)S(1)}, u32[]{:S(2)}, u32[]{:S(2)}) collective-permute-start(bf16[128,1280]{1,0:T(8,128)(2,1)S(1)} %get-tuple-element.80), channel_id=1, source_target_pairs={{0,16},{4,20},{8,24},{12,28},{16,0},{20,4},{24,8},{28,12},{1,17},{... | collective-permute-start | bytes 983048 | tf_op jit(solution)/shard_map/ppermute | solution.py:21
  91.9 5.2 %collective-permute-done.26 = bf16[128,1280]{1,0:T(8,128)(2,1)S(1)} collective-permute-done((bf16[128,1280]{1,0:T(8,128)(2,1)S(1)}, bf16[128,1280]{1,0:T(8,128)(2,1)S(1)}, u32[]{:S(2)}, u32[]{:S(2)}) %collective-permute-start.26) | collective-permute-done | bytes 327712 | tf_op jit(solution)/shard_map/ppermute | solution.py:21
  97.1 1.5 %collective-permute-done.27 = bf16[128,1280]{1,0:T(8,128)(2,1)S(1)} collective-permute-done((bf16[128,1280]{1,0:T(8,128)(2,1)S(1)}, bf16[128,1280]{1,0:T(8,128)(2,1)S(1)}, u32[]{:S(2)}, u32[]{:S(2)}) %collective-permute-start.27) | collective-permute-done | bytes 327712 | tf_op jit(solution)/shard_map/ppermute | solution.py:21
  99.8 4.3 %collective-permute-done.34 = bf16[128,1280]{1,0:T(8,128)(2,1)S(1)} collective-permute-done((bf16[128,1280]{1,0:T(8,128)(2,1)S(1)}, bf16[128,1280]{1,0:T(8,128)(2,1)S(1)}, u32[]{:S(2)}, u32[]{:S(2)}) %collective-permute-start.34) | collective-permute-done | bytes 327712 | tf_op jit(solution)/shard_map/ppermute | solution.py:21
  106.8 2.3 %collective-permute-done.28 = bf16[64,1280]{1,0:T(8,128)(2,1)S(1)} collective-permute-done((bf16[64,1280]{1,0:T(8,128)(2,1)S(1)}, bf16[64,1280]{1,0:T(8,128)(2,1)S(1)}, u32[]{:S(2)}, u32[]{:S(2)}) %collective-permute-start.28) | collective-permute-done | bytes 163872 | tf_op jit(solution)/shard_map/ppermute | solution.py:21
  109.3 2.5 %collective-permute-start.30 = (bf16[128,640]{1,0:T(8,128)(2,1)S(1)}, bf16[128,640]{1,0:T(8,128)(2,1)S(1)}, u32[]{:S(2)}, u32[]{:S(2)}) collective-permute-start(bf16[128,640]{1,0:T(8,128)(2,1)S(1)} %get-tuple-element.111), channel_id=1, source_target_pairs={{0,3},{1,2},{2,1},{3,0},{4,7},{5,6},{6,5},{7,4},{8,11},{9,10},{10,... | collective-permute-start | bytes 491528 | tf_op jit(solution)/shard_map/ppermute | solution.py:21
  111.9 2.5 %collective-permute-start.31 = (bf16[128,640]{1,0:T(8,128)(2,1)S(1)}, bf16[128,640]{1,0:T(8,128)(2,1)S(1)}, u32[]{:S(2)}, u32[]{:S(2)}) collective-permute-start(bf16[128,640]{1,0:T(8,128)(2,1)S(1)} %get-tuple-element.112), channel_id=1, source_target_pairs={{0,2},{1,3},{2,0},{3,1},{4,6},{5,7},{6,4},{7,5},{8,10},{9,11},{10,... | collective-permute-start | bytes 491528 | tf_op jit(solution)/shard_map/ppermute | solution.py:21
  115.1 2.7 %collective-permute-done.30 = bf16[128,640]{1,0:T(8,128)(2,1)S(1)} collective-permute-done((bf16[128,640]{1,0:T(8,128)(2,1)S(1)}, bf16[128,640]{1,0:T(8,128)(2,1)S(1)}, u32[]{:S(2)}, u32[]{:S(2)}) %collective-permute-start.30) | collective-permute-done | bytes 163872 | tf_op jit(solution)/shard_map/ppermute | solution.py:21
  117.8 7.8 %collective-permute-done.31 = bf16[128,640]{1,0:T(8,128)(2,1)S(1)} collective-permute-done((bf16[128,640]{1,0:T(8,128)(2,1)S(1)}, bf16[128,640]{1,0:T(8,128)(2,1)S(1)}, u32[]{:S(2)}, u32[]{:S(2)}) %collective-permute-start.31) | collective-permute-done | bytes 163872 | tf_op jit(solution)/shard_map/ppermute | solution.py:21
  (99 shorter events, 26.3 us)
Async XLA Ops:
  0.0 13.7 %collective-permute-start.1 = (bf16[128,640]{1,0:T(8,128)(2,1)}, bf16[128,640]{1,0:T(8,128)(2,1)S(1)}, u32[]{:S(2)}, u32[]{:S(2)}) collective-permute-start(bf16[128,640]{1,0:T(8,128)(2,1)} %param.11), channel_id=1, source_target_pairs={{0,2},{1,3},{2,0},{3,1},{4,6},{5,7},{6,4},{7,5},{8,10},{9,11},{10,... | collective-permute-start | bytes 491528 | tf_op jit(solution)/shard_map/ppermute | solution.py:21
  5.6 11.1 %collective-permute-start.2 = (bf16[128,640]{1,0:T(8,128)(2,1)}, bf16[128,640]{1,0:T(8,128)(2,1)S(1)}, u32[]{:S(2)}, u32[]{:S(2)}) collective-permute-start(bf16[128,640]{1,0:T(8,128)(2,1)} %param.11), channel_id=1, source_target_pairs={{0,3},{1,2},{2,1},{3,0},{4,7},{5,6},{6,5},{7,4},{8,11},{9,10},{10,... | collective-permute-start | bytes 491528 | tf_op jit(solution)/shard_map/ppermute | solution.py:21
  7.8 13.8 %collective-permute-start.23 = (bf16[320,384]{1,0:T(8,128)(2,1)S(1)}, bf16[320,384]{1,0:T(8,128)(2,1)S(1)}, u32[]{:S(2)}, u32[]{:S(2)}) collective-permute-start(bf16[320,384]{1,0:T(8,128)(2,1)S(1)} %get-tuple-element.89), channel_id=1, source_target_pairs={{0,28},{4,24},{8,20},{12,16},{16,12},{20,8},{24,4},{28,0},{1,29},{... | collective-permute-start | bytes 737288 | tf_op jit(solution)/shard_map/ppermute | solution.py:21
  18.0 11.0 %collective-permute-start.11 = (bf16[64,2688]{1,0:T(8,128)(2,1)S(1)}, bf16[64,2688]{1,0:T(8,128)(2,1)S(1)}, u32[]{:S(2)}, u32[]{:S(2)}) collective-permute-start(bf16[64,2688]{1,0:T(8,128)(2,1)S(1)} %get-tuple-element.105.refs_2_), channel_id=1, source_target_pairs={{0,8},{4,12},{8,0},{12,4},{16,24},{20,28},{24,16},{28,20},{1,9},{5... | collective-permute-start | bytes 1032200 | tf_op jit(solution)/shard_map/ppermute | solution.py:21
  19.5 10.9 %collective-permute-start.4 = (bf16[64,2688]{1,0:T(8,128)(2,1)S(1)}, bf16[64,2688]{1,0:T(8,128)(2,1)S(1)}, u32[]{:S(2)}, u32[]{:S(2)}) collective-permute-start(bf16[64,2688]{1,0:T(8,128)(2,1)S(1)} %get-tuple-element.105.refs_2_), channel_id=1, source_target_pairs={{0,16},{4,20},{8,24},{12,28},{16,0},{20,4},{24,8},{28,12},{1,17},{... | collective-permute-start | bytes 1032200 | tf_op jit(solution)/shard_map/ppermute | solution.py:21
  21.1 15.3 %collective-permute-start.3 = (bf16[64,2688]{1,0:T(8,128)(2,1)S(1)}, bf16[64,2688]{1,0:T(8,128)(2,1)S(1)}, u32[]{:S(2)}, u32[]{:S(2)}) collective-permute-start(bf16[64,2688]{1,0:T(8,128)(2,1)S(1)} %get-tuple-element.106.refs_0_), channel_id=1, source_target_pairs={{0,8},{4,12},{8,0},{12,4},{16,24},{20,28},{24,16},{28,20},{1,9},{5... | collective-permute-start | bytes 1032200 | tf_op jit(solution)/shard_map/ppermute | solution.py:21
  21.6 16.3 %collective-permute-start.9 = (bf16[64,2688]{1,0:T(8,128)(2,1)S(1)}, bf16[64,2688]{1,0:T(8,128)(2,1)S(1)}, u32[]{:S(2)}, u32[]{:S(2)}) collective-permute-start(bf16[64,2688]{1,0:T(8,128)(2,1)S(1)} %get-tuple-element.106.refs_0_), channel_id=1, source_target_pairs={{0,16},{4,20},{8,24},{12,28},{16,0},{20,4},{24,8},{28,12},{1,17},{... | collective-permute-start | bytes 1032200 | tf_op jit(solution)/shard_map/ppermute | solution.py:21
  29.0 14.5 %collective-permute-start.5 = (bf16[64,2688]{1,0:T(8,128)(2,1)S(1)}, bf16[64,2688]{1,0:T(8,128)(2,1)S(1)}, u32[]{:S(2)}, u32[]{:S(2)}) collective-permute-start(bf16[64,2688]{1,0:T(8,128)(2,1)S(1)} %get-tuple-element.106.refs_0_), channel_id=1, source_target_pairs={{0,4},{4,0},{8,12},{12,8},{16,20},{20,16},{24,28},{28,24},{1,5},{5... | collective-permute-start | bytes 1032200 | tf_op jit(solution)/shard_map/ppermute | solution.py:21
  30.5 14.5 %collective-permute-start.12 = (bf16[64,2688]{1,0:T(8,128)(2,1)S(1)}, bf16[64,2688]{1,0:T(8,128)(2,1)S(1)}, u32[]{:S(2)}, u32[]{:S(2)}) collective-permute-start(bf16[64,2688]{1,0:T(8,128)(2,1)S(1)} %collective-permute-done.4.refs_3_), channel_id=1, source_target_pairs={{0,8},{4,12},{8,0},{12,4},{16,24},{20,28},{24,16},{28,20},{1,9},{5... | collective-permute-start | bytes 1032200 | tf_op jit(solution)/shard_map/ppermute | solution.py:21
  31.0 14.2 %collective-permute-start.8 = (bf16[64,2688]{1,0:T(8,128)(2,1)S(1)}, bf16[64,2688]{1,0:T(8,128)(2,1)S(1)}, u32[]{:S(2)}, u32[]{:S(2)}) collective-permute-start(bf16[64,2688]{1,0:T(8,128)(2,1)S(1)} %collective-permute-done.4.refs_3_), channel_id=1, source_target_pairs={{0,4},{4,0},{8,12},{12,8},{16,20},{20,16},{24,28},{28,24},{1,5},{5... | collective-permute-start | bytes 1032200 | tf_op jit(solution)/shard_map/ppermute | solution.py:21
  43.5 10.8 %collective-permute-start.22 = (bf16[320,384]{1,0:T(8,128)(2,1)S(1)}, bf16[320,384]{1,0:T(8,128)(2,1)S(1)}, u32[]{:S(2)}, u32[]{:S(2)}) collective-permute-start(bf16[320,384]{1,0:T(8,128)(2,1)S(1)} %get-tuple-element.90), channel_id=1, source_target_pairs={{0,24},{4,28},{8,16},{12,20},{16,8},{20,12},{24,0},{28,4},{1,25},{... | collective-permute-start | bytes 737288 | tf_op jit(solution)/shard_map/ppermute | solution.py:21
  45.0 10.7 %collective-permute-start.15 = (bf16[64,2688]{1,0:T(8,128)(2,1)S(1)}, bf16[64,2688]{1,0:T(8,128)(2,1)S(1)}, u32[]{:S(2)}, u32[]{:S(2)}) collective-permute-start(bf16[64,2688]{1,0:T(8,128)(2,1)S(1)} %collective-permute-done.11.refs_2_), channel_id=1, source_target_pairs={{0,4},{4,0},{8,12},{12,8},{16,20},{20,16},{24,28},{28,24},{1,5},{5... | collective-permute-start | bytes 1032200 | tf_op jit(solution)/shard_map/ppermute | solution.py:21
  45.2 11.0 %collective-permute-start.13 = (bf16[64,2688]{1,0:T(8,128)(2,1)S(1)}, bf16[64,2688]{1,0:T(8,128)(2,1)S(1)}, u32[]{:S(2)}, u32[]{:S(2)}) collective-permute-start(bf16[64,2688]{1,0:T(8,128)(2,1)S(1)} %collective-permute-done.9.refs_0_), channel_id=1, source_target_pairs={{0,4},{4,0},{8,12},{12,8},{16,20},{20,16},{24,28},{28,24},{1,5},{5... | collective-permute-start | bytes 1032200 | tf_op jit(solution)/shard_map/ppermute | solution.py:21
  45.5 10.8 %collective-permute-start.16 = (bf16[64,2688]{1,0:T(8,128)(2,1)S(1)}, bf16[64,2688]{1,0:T(8,128)(2,1)S(1)}, u32[]{:S(2)}, u32[]{:S(2)}) collective-permute-start(bf16[64,2688]{1,0:T(8,128)(2,1)S(1)} %collective-permute-done.12.refs_3_), channel_id=1, source_target_pairs={{0,4},{4,0},{8,12},{12,8},{16,20},{20,16},{24,28},{28,24},{1,5},{5... | collective-permute-start | bytes 1032200 | tf_op jit(solution)/shard_map/ppermute | solution.py:21
  45.7 12.1 %collective-permute-start.14 = (bf16[64,2688]{1,0:T(8,128)(2,1)S(1)}, bf16[64,2688]{1,0:T(8,128)(2,1)S(1)}, u32[]{:S(2)}, u32[]{:S(2)}) collective-permute-start(bf16[64,2688]{1,0:T(8,128)(2,1)S(1)} %collective-permute-done.10.refs_1_), channel_id=1, source_target_pairs={{0,4},{4,0},{8,12},{12,8},{16,20},{20,16},{24,28},{28,24},{1,5},{5... | collective-permute-start | bytes 1032200 | tf_op jit(solution)/shard_map/ppermute | solution.py:21
  54.3 12.0 %collective-permute-start.21 = (bf16[320,384]{1,0:T(8,128)(2,1)S(1)}, bf16[320,384]{1,0:T(8,128)(2,1)S(1)}, u32[]{:S(2)}, u32[]{:S(2)}) collective-permute-start(bf16[320,384]{1,0:T(8,128)(2,1)S(1)} %get-tuple-element.91), channel_id=1, source_target_pairs={{0,20},{4,16},{8,28},{12,24},{16,4},{20,0},{24,12},{28,8},{1,21},{... | collective-permute-start | bytes 737288 | tf_op jit(solution)/shard_map/ppermute | solution.py:21
  55.7 12.2 %collective-permute-start.20 = (bf16[320,384]{1,0:T(8,128)(2,1)S(1)}, bf16[320,384]{1,0:T(8,128)(2,1)S(1)}, u32[]{:S(2)}, u32[]{:S(2)}) collective-permute-start(bf16[320,384]{1,0:T(8,128)(2,1)S(1)} %get-tuple-element.92), channel_id=1, source_target_pairs={{0,16},{4,20},{8,24},{12,28},{16,0},{20,4},{24,8},{28,12},{1,17},{... | collective-permute-start | bytes 737288 | tf_op jit(solution)/shard_map/ppermute | solution.py:21
  56.2 11.7 %collective-permute-start.19 = (bf16[320,384]{1,0:T(8,128)(2,1)S(1)}, bf16[320,384]{1,0:T(8,128)(2,1)S(1)}, u32[]{:S(2)}, u32[]{:S(2)}) collective-permute-start(bf16[320,384]{1,0:T(8,128)(2,1)S(1)} %get-tuple-element.93), channel_id=1, source_target_pairs={{0,12},{4,8},{8,4},{12,0},{16,28},{20,24},{24,20},{28,16},{1,13},{... | collective-permute-start | bytes 737288 | tf_op jit(solution)/shard_map/ppermute | solution.py:21
  56.3 13.4 %collective-permute-start.18 = (bf16[320,384]{1,0:T(8,128)(2,1)S(1)}, bf16[320,384]{1,0:T(8,128)(2,1)S(1)}, u32[]{:S(2)}, u32[]{:S(2)}) collective-permute-start(bf16[320,384]{1,0:T(8,128)(2,1)S(1)} %get-tuple-element.94), channel_id=1, source_target_pairs={{0,8},{4,12},{8,0},{12,4},{16,24},{20,28},{24,16},{28,20},{1,9},{5... | collective-permute-start | bytes 737288 | tf_op jit(solution)/shard_map/ppermute | solution.py:21
  57.8 11.9 %collective-permute-start.17 = (bf16[320,384]{1,0:T(8,128)(2,1)S(1)}, bf16[320,384]{1,0:T(8,128)(2,1)S(1)}, u32[]{:S(2)}, u32[]{:S(2)}) collective-permute-start(bf16[320,384]{1,0:T(8,128)(2,1)S(1)} %get-tuple-element.95), channel_id=1, source_target_pairs={{0,4},{4,0},{8,12},{12,8},{16,20},{20,16},{24,28},{28,24},{1,5},{5... | collective-permute-start | bytes 737288 | tf_op jit(solution)/shard_map/ppermute | solution.py:21
  89.5 14.6 %collective-permute-start.34 = (bf16[128,1280]{1,0:T(8,128)(2,1)S(1)}, bf16[128,1280]{1,0:T(8,128)(2,1)S(1)}, u32[]{:S(2)}, u32[]{:S(2)}) collective-permute-start(bf16[128,1280]{1,0:T(8,128)(2,1)S(1)} %get-tuple-element.80), channel_id=1, source_target_pairs={{0,16},{4,20},{8,24},{12,28},{16,0},{20,4},{24,8},{28,12},{1,17},{... | collective-permute-start | bytes 983048 | tf_op jit(solution)/shard_map/ppermute | solution.py:21
  91.1 14.5 %collective-permute-start.35 = (bf16[128,1280]{1,0:T(8,128)(2,1)S(1)}, bf16[128,1280]{1,0:T(8,128)(2,1)S(1)}, u32[]{:S(2)}, u32[]{:S(2)}) collective-permute-start(bf16[128,1280]{1,0:T(8,128)(2,1)S(1)} %get-tuple-element.81), channel_id=1, source_target_pairs={{0,8},{4,12},{8,0},{12,4},{16,24},{20,28},{24,16},{28,20},{1,9},{5... | collective-permute-start | bytes 983048 | tf_op jit(solution)/shard_map/ppermute | solution.py:21
  111.9 13.7 %collective-permute-start.31 = (bf16[128,640]{1,0:T(8,128)(2,1)S(1)}, bf16[128,640]{1,0:T(8,128)(2,1)S(1)}, u32[]{:S(2)}, u32[]{:S(2)}) collective-permute-start(bf16[128,640]{1,0:T(8,128)(2,1)S(1)} %get-tuple-element.112), channel_id=1, source_target_pairs={{0,2},{1,3},{2,0},{3,1},{4,6},{5,7},{6,4},{7,5},{8,10},{9,11},{10,... | collective-permute-start | bytes 491528 | tf_op jit(solution)/shard_map/ppermute | solution.py:21
  114.6 11.0 %collective-permute-start.38 = (bf16[128,640]{1,0:T(8,128)(2,1)S(1)}, bf16[128,640]{1,0:T(8,128)(2,1)S(1)}, u32[]{:S(2)}, u32[]{:S(2)}) collective-permute-start(bf16[128,640]{1,0:T(8,128)(2,1)S(1)} %fusion.1), channel_id=1, source_target_pairs={{0,1},{1,0},{2,3},{3,2},{4,5},{5,4},{6,7},{7,6},{8,9},{9,8},{10,11... | collective-permute-start | bytes 491528 | tf_op jit(solution)/shard_map/ppermute | solution.py:21
  (21 other events, 166.2 us)
where the time goes:
time: 127 us; the launch traced here: 126 us
  waiting for transfers between devices  50.1 us (39%)
  Pallas kernels  37.4 us (29%)
  starting transfers between devices  32.8 us (26%)
  local copies, waits for them, and re-layouts  3.18 us (3%)
  other arithmetic  1.94 us (2%)
    ppermute x39, waiting for transfers between devices, swap(): lax.ppermute(block, axis, [(i, i ^ bit) for i in range(lax.axis_size(axis...  50.1 us
    ppermute x39, starting transfers between devices, swap(): lax.ppermute(block, axis, [(i, i ^ bit) for i in range(lax.axis_size(axis...  32.8 us
    pallas_call x2, Pallas kernels, routed_hidden(): pl.pallas_call(functools.partial(hidden_kernel, n_pieces), out_shape=(plt...  16.4 us
    pallas_call x2, Pallas kernels, both_down(): pl.pallas_call(functools.partial(down_kernel, 0 if ready else len(strips)...  15.3 us
    pallas_call x1, Pallas kernels, stage(): pl.pallas_call(stage_kernel, out_shape=tuple((pltpu.VMEM(w.shape, BF16) f...  5.6 us
  transfers between devices with their start and end apart: 39, of which 15 were waited for; matrix products, arithmetic and copies ran while one was open for 3% of the time, Pallas kernels for 22%

commit v1 on v0

v1 whole, which is shorter than its diff:
```python
import functools

import jax
import jax.numpy as jnp
from jax import lax
from jax.experimental import pallas as pl
from jax.experimental.pallas import tpu as pltpu
from jax.sharding import PartitionSpec as P


F32, BF16 = jnp.float32, jnp.bfloat16
ROWS = 256
BLOCK = 512
ANY, VMEM = pl.BlockSpec(memory_space=pl.ANY), pl.BlockSpec(memory_space=pltpu.VMEM)
HBM, SMEM = pl.BlockSpec(memory_space=pltpu.HBM), pl.BlockSpec(memory_space=pltpu.SMEM)
DMA = pltpu.SemaphoreType.DMA
MIB = 1024 * 1024


def swap(block, axis, bit):
    return lax.ppermute(block, axis, [(i, i ^ bit) for i in range(lax.axis_size(axis))])


def tie(*values):
    return lax.optimization_barrier(values)


def orders(size):
    bits = [1 << k for k in range(1, size.bit_length() - 1)]
    turn = len(bits) // 2
    return bits, bits[turn:] + bits[:turn]


def silu(v):
    return v / (1.0 + jnp.exp(-v))


def cost(flops, bytes_accessed):
    return pl.CostEstimate(flops=flops, bytes_accessed=bytes_accessed, transcendentals=0)


def assemble_kernel(n_cuts, meta, *refs):
    features, names, outs = refs[:n_cuts], refs[n_cuts], refs[n_cuts + 1 :]
    depth = features[0].shape[1]
    half = outs[0].shape[0]
    for h, out in enumerate(outs):
        rows = slice(h * half, (h + 1) * half)
        out[:, n_cuts * depth :] = names[rows]
        for k, feature in enumerate(features):
            out[:, pl.ds(pl.multiple_of(meta[1 + n_cuts - k], 128), depth)] = feature[rows]


def assemble(meta, features, names):
    n_cuts, (rows, depth) = len(features), features[0].shape
    out = pltpu.VMEM((rows // 2, n_cuts * depth + names.shape[1]), BF16)
    return pl.pallas_call(
        functools.partial(assemble_kernel, n_cuts),
        out_shape=(out, out),
        in_specs=[SMEM] + [VMEM] * (n_cuts + 1),
        out_specs=(VMEM, VMEM),
        compiler_params=pltpu.CompilerParams(vmem_limit_bytes=2 * MIB),
        cost_estimate=cost(10**6, 4 * n_cuts * rows * depth),
        name="assemble",
    )(meta, *features, names)


def stage_kernel(*refs):
    n = len(refs) // 2
    sources, targets, sems = refs[:n], refs[n : 2 * n], refs[2 * n]
    copies = [pltpu.make_async_copy(s, t, sems.at[i]) for i, (s, t) in enumerate(zip(sources, targets))]
    for copy in copies:
        copy.start()
    for copy in copies:
        copy.wait()


def stage(weights):
    return pl.pallas_call(
        stage_kernel,
        out_shape=tuple(pltpu.VMEM(w.shape, BF16) for w in weights),
        in_specs=[HBM] * len(weights),
        out_specs=(VMEM,) * len(weights),
        scratch_shapes=[DMA((len(weights),))],
        compiler_params=pltpu.CompilerParams(vmem_limit_bytes=42 * MIB),
        cost_estimate=cost(5 * 10**9, 2 * sum(w.size for w in weights)),
        name="stage",
    )(*weights)


def hidden_kernel(n_pieces, meta, *refs):
    pieces, (router, gate, up, hidden, x) = refs[:n_pieces], refs[n_pieces:]
    width, units = gate.shape[1:]
    span = pieces[0].shape[0]
    for i, piece in enumerate(pieces):
        x[i * span : (i + 1) * span, :] = piece[...]
    batch = x[:, :width]
    slots = x[:, width : width + 1].astype(F32)
    home = jnp.floor(slots * 0.5)
    chosen = jnp.where(slots == 2.0 * home, home, meta[1].astype(F32)) == meta[0].astype(F32)
    logits = lax.dot_general(batch, router[...], (((1,), (1,)), ((), ())), preferred_element_type=F32)
    column = lax.broadcasted_iota(jnp.int32, logits.shape, 1) == meta[0]
    logit = jnp.sum(jnp.where(column, logits, 0.0), axis=1, keepdims=True)
    weighting = jnp.where(chosen, 1.0 / (1.0 + jnp.exp(-logit)), 0.0)
    block = min(BLOCK, units)
    for at in range(0, units, block):
        lanes = slice(at, at + block)
        gated = jnp.dot(batch, gate[0, :, lanes], preferred_element_type=F32)
        upward = jnp.dot(batch, up[0, :, lanes], preferred_element_type=F32)
        hidden[:, lanes] = (silu(gated) * upward * weighting).astype(BF16)


def routed_hidden(meta, pieces, weights):
    n_pieces = len(pieces)
    rows, across = n_pieces * pieces[0].shape[0], pieces[0].shape[1]
    width, units = weights[1].shape[1:]
    return pl.pallas_call(
        functools.partial(hidden_kernel, n_pieces),
        out_shape=(pltpu.VMEM((rows, units), BF16), pltpu.VMEM((rows, across), BF16)),
        in_specs=[SMEM] + [VMEM] * (n_pieces + 3),
        out_specs=(VMEM, VMEM),
        compiler_params=pltpu.CompilerParams(vmem_limit_bytes=10 * MIB),
        cost_estimate=cost(4 * rows * width * units, 4 * width * units),
        name="routed_hidden",
    )(meta, *pieces, *weights[:3])


def shared_units(p_s, batches, hiddens):
    cols = p_s.shape[1] // 3
    for batch, hidden in zip(batches, hiddens):
        both = jnp.dot(batch[:, : p_s.shape[0]], p_s[:, : 2 * cols], preferred_element_type=F32)
        hidden[...] = (silu(both[:, :cols]) * both[:, cols:]).astype(BF16)


def more_kernel(n_batches, p_s, *refs):
    shared_units(p_s, refs[:n_batches], refs[n_batches:])


def more_hidden(packed, batches):
    rows, (width, cols) = batches[0].shape[0], packed.shape
    return pl.pallas_call(
        functools.partial(more_kernel, len(batches)),
        out_shape=(pltpu.VMEM((rows, cols // 3), BF16),) * len(batches),
        in_specs=[VMEM] * (1 + len(batches)),
        out_specs=(VMEM,) * len(batches),
        compiler_params=pltpu.CompilerParams(vmem_limit_bytes=6 * MIB),
        cost_estimate=cost(2 * rows * width * cols * len(batches), 2 * width * cols),
        name="more_hidden",
    )(packed, *batches)


def prep_kernel(n_strips, n_batches, n_cuts, meta, *refs):
    strips, batches, refs = refs[:n_strips], refs[n_strips : n_strips + n_batches], refs[n_strips + n_batches :]
    turned, p_s, *hiddens, sem = refs
    width = p_s.shape[0]
    depth = width // n_cuts
    cols = turned.shape[1]
    strip = strips[0].shape[0]
    rows_of = [pl.ds(pl.multiple_of(meta[2 + n_cuts + j], 16), strip) for j in range(n_strips)]
    loads = [pltpu.make_async_copy(s, p_s.at[rows_of[j], :], sem.at[j]) for j, s in enumerate(strips)]
    for copy in loads:
        copy.start()
    for copy in loads:
        copy.wait()
    shared_units(p_s, batches, hiddens)
    for k in range(n_cuts):
        turned[k] = jnp.transpose(p_s[pl.ds(pl.multiple_of(meta[2 + k], 128), depth), 2 * cols :], (1, 0))


def shared_hidden(meta, strips, batches, width, n_cuts):
    cols = strips[0].shape[1] // 3
    rows = batches[0].shape[0]
    return pl.pallas_call(
        functools.partial(prep_kernel, len(strips), len(batches), n_cuts),
        out_shape=(pltpu.VMEM((n_cuts, cols, width // n_cuts), BF16), pltpu.VMEM((width, 3 * cols), BF16))
        + (pltpu.VMEM((rows, cols), BF16),) * len(batches),
        in_specs=[SMEM] + [ANY] * len(strips) + [VMEM] * len(batches),
        out_specs=(VMEM,) * (2 + len(batches)),
        scratch_shapes=[DMA((len(strips),))],
        compiler_params=pltpu.CompilerParams(vmem_limit_bytes=8 * MIB),
        cost_estimate=cost(8 * rows * width * cols * len(batches), 6 * width * cols),
        name="shared_hidden",
    )(meta, *strips, *batches)


def down_kernel(n_batches, part, n_cuts, meta, down, turned, *refs):
    hiddens, shareds, (kept, sent) = refs[:n_batches], refs[n_batches : 2 * n_batches], refs[2 * n_batches :]
    depth = down.shape[2] // n_cuts
    n_kept = hiddens[0].shape[0] // 2
    for i in range(n_cuts // 2):
        k = part * n_cuts // 2 + i
        place = pl.ds(pl.multiple_of(meta[2 + k], 128), depth)
        here = slice(i * depth, (i + 1) * depth)
        for n, (hidden, shared) in enumerate(zip(hiddens, shareds)):
            total = jnp.dot(hidden[...], down[0, :, place], preferred_element_type=F32)
            total = total + jnp.dot(shared[...], turned[k], preferred_element_type=F32)
            kept[n * n_kept : (n + 1) * n_kept, here] = total[:n_kept]
            sent[n * n_kept : (n + 1) * n_kept, here] = total[n_kept:].astype(BF16)


def both_down(meta, hiddens, shareds, down, turned, part, n_cuts):
    (rows, units), width = hiddens[0].shape, down.shape[2]
    rows *= len(hiddens)
    return pl.pallas_call(
        functools.partial(down_kernel, len(hiddens), part, n_cuts),
        out_shape=(pltpu.VMEM((rows // 2, width // 2), F32), pltpu.VMEM((rows // 2, width // 2), BF16)),
        in_specs=[SMEM] + [VMEM] * (2 + 2 * len(hiddens)),
        out_specs=(VMEM, VMEM),
        compiler_params=pltpu.CompilerParams(vmem_limit_bytes=6 * MIB),
        cost_estimate=cost(rows * width * (units + shareds[0].shape[1]), width * units),
        name="both_down",
    )(meta, down, turned, *hiddens, *shareds)


def local(
    tokens,
    slot,
    mask,
    hot_group,
    router_weight,
    exp_gate,
    exp_up,
    exp_down,
    sh_gate,
    sh_up,
    sh_down,
):
    n_groups, n_cuts = lax.axis_size("expert"), lax.axis_size("tensor")
    me, cut = lax.axis_index("expert"), lax.axis_index("tensor")
    rows, depth = tokens.shape
    half = rows // 2
    strip, cols = sh_gate.shape[0], sh_gate.shape[1] // n_groups
    relative = list(range(n_cuts))[::-1]
    numbers = [me, hot_group[0]] + [(cut ^ k) * depth for k in relative]
    numbers += [(me ^ j) * strip for j in range(n_groups)]
    meta = jnp.stack(numbers).astype(jnp.int32)

    features = [tokens] + [swap(tokens, "tensor", k) for k in range(1, n_cuts)]
    names = jnp.broadcast_to(slot.astype(BF16), (rows, 128))
    real = mask.astype(F32)[:, None]

    packed = jnp.concatenate(
        [
            sh_gate.reshape(strip, n_groups, cols).transpose(1, 0, 2),
            sh_up.reshape(strip, n_groups, cols).transpose(1, 0, 2),
            sh_down.reshape(n_groups, cols, strip).transpose(0, 2, 1),
        ],
        axis=2,
    )
    blocks = [lax.dynamic_index_in_dim(packed, me ^ j, 0, keepdims=False) for j in range(n_groups)]
    far_first = sorted(range(1, n_groups), key=lambda j: (-(j >> 1).bit_count(), j))
    soon, rest = far_first[: n_groups // 4], far_first[n_groups // 4 :]
    strips = {0: blocks[0]}
    strips.update({j: swap(blocks[j], "expert", j) for j in soon})

    router = router_weight.T
    names, real, meta, router, _ = tie(names, real, meta, router, blocks)
    weights = stage((router, exp_gate, exp_up, exp_down))
    halves = assemble(meta, features, names)

    routes = orders(n_groups)
    last = len(routes[0]) - 1

    def cross(pieces, phase):
        return [{j | r[phase]: swap(b, "expert", r[phase]) for j, b in p.items()} for r, p in zip(routes, pieces)]

    def join(*groups):
        return [{j: b for g in groups for j, b in g[h].items()} for h in (0, 1)]

    def with_mates(pieces):
        return join(pieces, [{j | 1: swap(b, "expert", 1) for j, b in p.items()} for p in pieces])

    own = [{0: piece} for piece in halves]
    parts = {"zero": with_mates(own)}
    came = [{}, {}]
    for phase in range(last):
        came = join(came, cross(join(own, came), phase))
    straight = cross(own, last)
    parts["one"] = with_mates(came)
    parts["two"] = with_mates(straight)
    parts["three"] = with_mates(cross(came, last))
    strips.update({j: swap(blocks[j], "expert", j) for j in rest})
    strips = [strips[j] for j in range(n_groups)]

    begun = {"late": [], "early": []}
    for name, part in parts.items():
        even = [(h, j) for h in (0, 1) for j in sorted(part[h]) if j & 1 == 0]
        many = min(len(even), ROWS // (2 * half))
        for at in range(0, len(even), many):
            stay = even[at : at + many]
            batch = [part[h][j] for h, j in stay] + [part[h][j | 1] for h, j in stay]
            done = routed_hidden(meta, batch, weights)
            begun["late" if name in ("two", "three") else "early"].append((stay, *done))

    acc = [[{}, {}], [{}, {}]]
    turned, held, *shared = shared_hidden(meta, strips, [x for _, _, x in begun["late"]], depth * n_cuts, n_cuts)
    shareds = {"late": shared}
    shareds["early"] = more_hidden(held, [x for _, _, x in begun["early"]])
    for name, some in begun.items():
        for c in (0, 1):
            kept, sent = both_down(meta, [h for _, h, _ in some], shareds[name], weights[3], turned, c, n_cuts)
            total = kept + swap(sent, "expert", 1).astype(F32)
            for i, (h, j) in enumerate(place for stay, _, _ in some for place in stay):
                acc[c][h][j] = total[i * half : (i + 1) * half]

    for phase in reversed(range(last + 1)):
        for c in (0, 1):
            away = [[j for j in a if j & r[phase]] for r, a in zip(routes, acc[c])]
            sends = [jnp.concatenate([a.pop(j) for j in js], axis=0).astype(BF16) for a, js in zip(acc[c], away)]
            came = tie(*[swap(send, "expert", r[phase]) for r, send in zip(routes, tie(*sends))])
            for r, a, js, got in zip(routes, acc[c], away, came):
                for i, j in enumerate(js):
                    a[j ^ r[phase]] = a[j ^ r[phase]] + got[i * half : (i + 1) * half].astype(F32)
    mixed = None
    for c in (0, 1):
        mine = jnp.concatenate([a[0] for a in acc[c]], axis=0)
        for i, k in enumerate(relative[c * n_cuts // 2 : (c + 1) * n_cuts // 2]):
            part = mine[:, i * depth : (i + 1) * depth]
            if k:
                part = swap(part.astype(BF16), "tensor", k).astype(F32)
            mixed = part if mixed is None else mixed + part
    return (mixed * real).astype(BF16)


def solution(mesh):
    in_specs = (
        P("expert", "tensor"),
        P("expert", None),
        P("expert"),
        P(),
        P(),
        P("expert", None, "tensor"),
        P("expert", None, "tensor"),
        P("expert", "tensor", None),
        P("expert", "tensor"),
        P("expert", "tensor"),
        P("tensor", "expert"),
    )
    out_specs = P("expert", "tensor")
    return jax.shard_map(local, mesh=mesh, in_specs=in_specs, out_specs=out_specs, check_vma=False)
```

time: 127 us -> 142 us (1.12)
  waiting for transfers between devices: 50.1 us -> 57.7 us
  starting transfers between devices: 32.8 us -> 39 us
  other arithmetic: 1.94 us -> 3.37 us
    ppermute x39, waiting for transfers between devices: 50.1 us -> 57.7 us  [swap(): lax.ppermute(block, axis, [(i, i ^ bit) for i in range(lax.axis_size(axis...]
    ppermute x39, starting transfers between devices: 32.8 us -> 39 us  [swap(): lax.ppermute(block, axis, [(i, i ^ bit) for i in range(lax.axis_size(axis...]
    pallas_call x2 -> x7, Pallas kernels: 15.3 us -> 16.6 us  [the longest x4 10.8 us: both_down(): pl.pallas_call(functools.partial(down_kernel, len(hiddens), part, n_cuts)...]
    pallas_call x2 -> x4, Pallas kernels: 16.4 us -> 15.7 us  [routed_hidden(): pl.pallas_call(functools.partial(hidden_kernel, n_pieces), out_shape=(plt...]
  transfers between devices with their start and end apart: 39 -> 39, of which waited for: 15 -> 16; matrix products, arithmetic and copies ran while one was open for 3% -> 4% of each run, Pallas kernels for 22% -> 26%
where the time goes in v1:
time: 142 us
  waiting for transfers between devices  57.7 us (41%)
  starting transfers between devices  39 us (27%)
  Pallas kernels  37.8 us (27%)
  other arithmetic  3.37 us (2%)
  local copies, waits for them, and re-layouts  3.03 us (2%)
    ppermute x39, waiting for transfers between devices, swap(): lax.ppermute(block, axis, [(i, i ^ bit) for i in range(lax.axis_size(axis...  57.7 us
    ppermute x39, starting transfers between devices, swap(): lax.ppermute(block, axis, [(i, i ^ bit) for i in range(lax.axis_size(axis...  39 us
    pallas_call x4, Pallas kernels, routed_hidden(): pl.pallas_call(functools.partial(hidden_kernel, n_pieces), out_shape=(plt...  15.7 us
    pallas_call x4, Pallas kernels, both_down(): pl.pallas_call(functools.partial(down_kernel, len(hiddens), part, n_cuts)...  10.8 us
    pallas_call x1, Pallas kernels, stage(): pl.pallas_call(stage_kernel, out_shape=tuple((pltpu.VMEM(w.shape, BF16) f...  5.6 us
    pallas_call x1, Pallas kernels, shared_hidden(): pl.pallas_call(functools.partial(prep_kernel, len(strips), len(batches),...  4.28 us
  transfers between devices with their start and end apart: 39, of which 16 were waited for; matrix products, arithmetic and copies ran while one was open for 4% of the time, Pallas kernels for 26%

profile of v1, /device:TPU:0, one launch (start us, length us, event | category | flops | bytes accessed | tf_op | source)
XLA Modules:
  0.0 142.0 jit_solution(14630090628429352218)
XLA Ops:
  0.0 3.1 %collective-permute-start.7 = (bf16[128,640]{1,0:T(8,128)(2,1)}, bf16[128,640]{1,0:T(8,128)(2,1)S(1)}, u32[]{:S(2)}, u32[]{:S(2)}) collective-permute-start(bf16[128,640]{1,0:T(8,128)(2,1)} %refs_0_.1), channel_id=1, source_target_pairs={{0,1},{1,0},{2,3},{3,2},{4,5},{5,4},{6,7},{7,6},{8,9},{9,8},{10,11... | collective-permute-start | bytes 491528 | tf_op jit(solution)/shard_map/ppermute | solution.py:21
  3.1 2.6 %collective-permute-start.8 = (bf16[128,640]{1,0:T(8,128)(2,1)}, bf16[128,640]{1,0:T(8,128)(2,1)S(1)}, u32[]{:S(2)}, u32[]{:S(2)}) collective-permute-start(bf16[128,640]{1,0:T(8,128)(2,1)} %refs_0_.1), channel_id=1, source_target_pairs={{0,2},{1,3},{2,0},{3,1},{4,6},{5,7},{6,4},{7,5},{8,10},{9,11},{10,... | collective-permute-start | bytes 491528 | tf_op jit(solution)/shard_map/ppermute | solution.py:21
  10.9 7.4 %collective-permute-done.8.refs_2_ = bf16[128,640]{1,0:T(8,128)(2,1)S(1)} collective-permute-done((bf16[128,640]{1,0:T(8,128)(2,1)}, bf16[128,640]{1,0:T(8,128)(2,1)S(1)}, u32[]{:S(2)}, u32[]{:S(2)}) %collective-permute-start.8) | collective-permute-done | bytes 163872 | tf_op jit(solution)/shard_map/ppermute | solution.py:21
  23.0 6.9 %collective-permute-done.10.refs_0_ = bf16[64,2688]{1,0:T(8,128)(2,1)S(1)} collective-permute-done((bf16[64,2688]{1,0:T(8,128)(2,1)S(1)}, bf16[64,2688]{1,0:T(8,128)(2,1)S(1)}, u32[]{:S(2)}, u32[]{:S(2)}) %collective-permute-start.10) | collective-permute-done | bytes 344096 | tf_op jit(solution)/shard_map/ppermute | solution.py:21
  31.3 3.7 %collective-permute-done.14.refs_0_ = bf16[64,2688]{1,0:T(8,128)(2,1)S(1)} collective-permute-done((bf16[64,2688]{1,0:T(8,128)(2,1)S(1)}, bf16[64,2688]{1,0:T(8,128)(2,1)S(1)}, u32[]{:S(2)}, u32[]{:S(2)}) %collective-permute-start.14) | collective-permute-done | bytes 344096 | tf_op jit(solution)/shard_map/ppermute | solution.py:21
  37.0 5.6 %stage.1 = (bf16[8,2560]{1,0:T(8,128)(2,1)S(1)}, bf16[1,2560,1024]{2,1,0:T(8,128)(2,1)S(1)}, bf16[1,2560,1024]{2,1,0:T(8,128)(2,1)S(1)}, bf16[1,1024,2560]{2,1,0:T(8,128)(2,1)S(1)}) custom-call(bf16[8,2560]{1,0:T(8,128)(2,1)} %bitcast.57, bf16[1,2560,1024]{2,1,0:T(8,128)(2,1)} %refs_1_.1, bf16[1,2560,1024]{2,1,0:T(8,128)(2,1)} %refs_2_.1, ...), custom_call_target="tpu_custom_call" | custom-call | flops 5000000000 | bytes 15769600 | tf_op jit(solution)/shard_map/stage/pallas_call | solution.py:78
  42.7 2.8 %collective-permute-done.15.refs_0_ = bf16[64,2688]{1,0:T(8,128)(2,1)S(1)} collective-permute-done((bf16[64,2688]{1,0:T(8,128)(2,1)S(1)}, bf16[64,2688]{1,0:T(8,128)(2,1)S(1)}, u32[]{:S(2)}, u32[]{:S(2)}) %collective-permute-start.15) | collective-permute-done | bytes 344096 | tf_op jit(solution)/shard_map/ppermute | solution.py:21
  46.0 3.9 %routed_hidden.6 = (bf16[256,1024]{1,0:T(8,128)(2,1)S(1)}, bf16[256,2688]{1,0:T(8,128)(2,1)S(1)}) custom-call(s32[14]{0:T(128)S(1)} %stack.55.meta, bf16[64,2688]{1,0:T(8,128)(2,1)S(1)} %get-tuple-element.57.refs_0_, bf16[64,2688]{1,0:T(8,128)(2,1)S(1)} %get-tuple-element.58.refs_1_, bf16[64,2688]{1,0:T(8,128)(2,1)S(1)} %collective-permute-done.20.refs_2_, ...), custom_call_target="tpu_custom_call" | custom-call | flops 2684354560 | bytes 10485760 | tf_op jit(solution)/shard_map/routed_hidden/pallas_call | solution.py:116
  53.1 3.9 %routed_hidden.4 = (bf16[256,1024]{1,0:T(8,128)(2,1)S(1)}, bf16[256,2688]{1,0:T(8,128)(2,1)S(1)}) custom-call(s32[14]{0:T(128)S(1)} %stack.55.meta, bf16[64,2688]{1,0:T(8,128)(2,1)S(1)} %collective-permute-done.10.refs_0_, bf16[64,2688]{1,0:T(8,128)(2,1)S(1)} %collective-permute-done.11.refs_1_, bf16[64,2688]{1,0:T(8,128)(2,1)S(1)} %collective-permute-done.12.refs_2_, ...), custom_call_target="tpu_custom_call" | custom-call | flops 2684354560 | bytes 10485760 | tf_op jit(solution)/shard_map/routed_hidden/pallas_call | solution.py:116
  58.8 3.7 %collective-permute-done.2.refs_3_ = bf16[320,384]{1,0:T(8,128)(2,1)S(1)} collective-permute-done((bf16[320,384]{1,0:T(8,128)(2,1)S(1)}, bf16[320,384]{1,0:T(8,128)(2,1)S(1)}, u32[]{:S(2)}, u32[]{:S(2)}) %collective-permute-start.2) | collective-permute-done | bytes 245792 | tf_op jit(solution)/shard_map/ppermute | solution.py:21
  62.6 2.7 %collective-permute-start.5 = (bf16[320,384]{1,0:T(8,128)(2,1)S(1)}, bf16[320,384]{1,0:T(8,128)(2,1)S(1)}, u32[]{:S(2)}, u32[]{:S(2)}) collective-permute-start(bf16[320,384]{1,0:T(8,128)(2,1)S(1)} %copy-done.4), channel_id=1, source_target_pairs={{0,24},{4,28},{8,16},{12,20},{16,8},{20,12},{24,0},{28,4},{1,25},{... | collective-permute-start | bytes 737288 | tf_op jit(solution)/shard_map/ppermute | solution.py:21
  66.2 3.9 %routed_hidden.5 = (bf16[256,1024]{1,0:T(8,128)(2,1)S(1)}, bf16[256,2688]{1,0:T(8,128)(2,1)S(1)}) custom-call(s32[14]{0:T(128)S(1)} %stack.55.meta, bf16[64,2688]{1,0:T(8,128)(2,1)S(1)} %collective-permute-done.15.refs_0_, bf16[64,2688]{1,0:T(8,128)(2,1)S(1)} %collective-permute-done.17.refs_1_, bf16[64,2688]{1,0:T(8,128)(2,1)S(1)} %collective-permute-done.18.refs_2_, ...), custom_call_target="tpu_custom_call" | custom-call | flops 2684354560 | bytes 10485760 | tf_op jit(solution)/shard_map/routed_hidden/pallas_call | solution.py:116
  72.3 5.1 %collective-permute-done.6.refs_7_ = bf16[320,384]{1,0:T(8,128)(2,1)S(1)} collective-permute-done((bf16[320,384]{1,0:T(8,128)(2,1)S(1)}, bf16[320,384]{1,0:T(8,128)(2,1)S(1)}, u32[]{:S(2)}, u32[]{:S(2)}) %collective-permute-start.6) | collective-permute-done | bytes 245792 | tf_op jit(solution)/shard_map/ppermute | solution.py:21
  77.4 4.3 %shared_hidden.1 = (bf16[4,128,640]{2,1,0:T(8,128)(2,1)S(1)}, bf16[2560,384]{1,0:T(8,128)(2,1)S(1)}, bf16[256,128]{1,0:T(8,128)(2,1)S(1)}, bf16[256,128]{1,0:T(8,128)(2,1)S(1)}) custom-call(s32[14]{0:T(128)S(1)} %stack.55.meta, bf16[320,384]{1,0:T(8,128)(2,1)S(1)} %get-tuple-element.108.refs_0_, bf16[320,384]{1,0:T(8,128)(2,1)S(1)} %collective-permute-done.refs_1_, ...), custom_call_target="tpu_custom_call" | custom-call | flops 1342177280 | bytes 1966080 | tf_op jit(solution)/shard_map/shared_hidden/pallas_call | solution.py:172
  81.7 2.7 %both_down.7 = (f32[256,1280]{1,0:T(8,128)S(1)}, bf16[256,1280]{1,0:T(8,128)(2,1)S(1)}) custom-call(s32[14]{0:T(128)S(1)} %stack.55.meta, bf16[1,1024,2560]{2,1,0:T(8,128)(2,1)S(1)} %get-tuple-element.55.down, bf16[4,128,640]{2,1,0:T(8,128)(2,1)S(1)} %get-tuple-element.64.turned, bf16[256,1024]{1,0:T(8,128)(2,1)S(1)} %get-tuple-element.74.refs_0_, ...), custom_call_target="tpu_custom_call" | custom-call | flops 1509949440 | bytes 2621440 | tf_op jit(solution)/shard_map/both_down/pallas_call | solution.py:203
  84.6 3.9 %routed_hidden.7 = (bf16[256,1024]{1,0:T(8,128)(2,1)S(1)}, bf16[256,2688]{1,0:T(8,128)(2,1)S(1)}) custom-call(s32[14]{0:T(128)S(1)} %stack.55.meta, bf16[64,2688]{1,0:T(8,128)(2,1)S(1)} %collective-permute-done.14.refs_0_, bf16[64,2688]{1,0:T(8,128)(2,1)S(1)} %collective-permute-done.16.refs_1_, bf16[64,2688]{1,0:T(8,128)(2,1)S(1)} %collective-permute-done.22.refs_2_, ...), custom_call_target="tpu_custom_call" | custom-call | flops 2684354560 | bytes 10485760 | tf_op jit(solution)/shard_map/routed_hidden/pallas_call | solution.py:116
  89.4 2.7 %both_down.6 = (f32[256,1280]{1,0:T(8,128)S(1)}, bf16[256,1280]{1,0:T(8,128)(2,1)S(1)}) custom-call(s32[14]{0:T(128)S(1)} %stack.55.meta, bf16[1,1024,2560]{2,1,0:T(8,128)(2,1)S(1)} %get-tuple-element.55.down, bf16[4,128,640]{2,1,0:T(8,128)(2,1)S(1)} %get-tuple-element.64.turned, bf16[256,1024]{1,0:T(8,128)(2,1)S(1)} %get-tuple-element.65.refs_0_, ...), custom_call_target="tpu_custom_call" | custom-call | flops 1509949440 | bytes 2621440 | tf_op jit(solution)/shard_map/both_down/pallas_call | solution.py:203
  92.6 2.7 %both_down.4 = (f32[256,1280]{1,0:T(8,128)S(1)}, bf16[256,1280]{1,0:T(8,128)(2,1)S(1)}) custom-call(s32[14]{0:T(128)S(1)} %stack.55.meta, bf16[1,1024,2560]{2,1,0:T(8,128)(2,1)S(1)} %get-tuple-element.55.down, bf16[4,128,640]{2,1,0:T(8,128)(2,1)S(1)} %get-tuple-element.64.turned, bf16[256,1024]{1,0:T(8,128)(2,1)S(1)} %get-tuple-element.65.refs_0_, ...), custom_call_target="tpu_custom_call" | custom-call | flops 1509949440 | bytes 2621440 | tf_op jit(solution)/shard_map/both_down/pallas_call | solution.py:203
  95.4 2.7 %both_down.5 = (f32[256,1280]{1,0:T(8,128)S(1)}, bf16[256,1280]{1,0:T(8,128)(2,1)S(1)}) custom-call(s32[14]{0:T(128)S(1)} %stack.55.meta, bf16[1,1024,2560]{2,1,0:T(8,128)(2,1)S(1)} %get-tuple-element.55.down, bf16[4,128,640]{2,1,0:T(8,128)(2,1)S(1)} %get-tuple-element.64.turned, bf16[256,1024]{1,0:T(8,128)(2,1)S(1)} %get-tuple-element.74.refs_0_, ...), custom_call_target="tpu_custom_call" | custom-call | flops 1509949440 | bytes 2621440 | tf_op jit(solution)/shard_map/both_down/pallas_call | solution.py:203
  103.7 5.8 %collective-permute-done.34 = bf16[128,1280]{1,0:T(8,128)(2,1)S(1)} collective-permute-done((bf16[128,1280]{1,0:T(8,128)(2,1)S(1)}, bf16[128,1280]{1,0:T(8,128)(2,1)S(1)}, u32[]{:S(2)}, u32[]{:S(2)}) %collective-permute-start.34) | collective-permute-done | bytes 327712 | tf_op jit(solution)/shard_map/ppermute | solution.py:21
  113.1 3.4 %collective-permute-done.26 = bf16[128,1280]{1,0:T(8,128)(2,1)S(1)} collective-permute-done((bf16[128,1280]{1,0:T(8,128)(2,1)S(1)}, bf16[128,1280]{1,0:T(8,128)(2,1)S(1)}, u32[]{:S(2)}, u32[]{:S(2)}) %collective-permute-start.26) | collective-permute-done | bytes 327712 | tf_op jit(solution)/shard_map/ppermute | solution.py:21
  121.4 4.1 %collective-permute-start.38 = (bf16[128,640]{1,0:T(8,128)(2,1)S(1)}, bf16[128,640]{1,0:T(8,128)(2,1)S(1)}, u32[]{:S(2)}, u32[]{:S(2)}) collective-permute-start(bf16[128,640]{1,0:T(8,128)(2,1)S(1)} %fusion.1), channel_id=1, source_target_pairs={{0,1},{1,0},{2,3},{3,2},{4,5},{5,4},{6,7},{7,6},{8,9},{9,8},{10,11... | collective-permute-start | bytes 491528 | tf_op jit(solution)/shard_map/ppermute | solution.py:21
  125.7 4.5 %collective-permute-start.31 = (bf16[128,640]{1,0:T(8,128)(2,1)S(1)}, bf16[128,640]{1,0:T(8,128)(2,1)S(1)}, u32[]{:S(2)}, u32[]{:S(2)}) collective-permute-start(bf16[128,640]{1,0:T(8,128)(2,1)S(1)} %get-tuple-element.126), channel_id=1, source_target_pairs={{0,2},{1,3},{2,0},{3,1},{4,6},{5,7},{6,4},{7,5},{8,10},{9,11},{10,... | collective-permute-start | bytes 491528 | tf_op jit(solution)/shard_map/ppermute | solution.py:21
  131.4 9.8 %collective-permute-done.31 = bf16[128,640]{1,0:T(8,128)(2,1)S(1)} collective-permute-done((bf16[128,640]{1,0:T(8,128)(2,1)S(1)}, bf16[128,640]{1,0:T(8,128)(2,1)S(1)}, u32[]{:S(2)}, u32[]{:S(2)}) %collective-permute-start.31) | collective-permute-done | bytes 163872 | tf_op jit(solution)/shard_map/ppermute | solution.py:21
  (112 shorter events, 39.1 us)
Async XLA Ops:
  0.0 10.9 %collective-permute-start.7 = (bf16[128,640]{1,0:T(8,128)(2,1)}, bf16[128,640]{1,0:T(8,128)(2,1)S(1)}, u32[]{:S(2)}, u32[]{:S(2)}) collective-permute-start(bf16[128,640]{1,0:T(8,128)(2,1)} %refs_0_.1), channel_id=1, source_target_pairs={{0,1},{1,0},{2,3},{3,2},{4,5},{5,4},{6,7},{7,6},{8,9},{9,8},{10,11... | collective-permute-start | bytes 491528 | tf_op jit(solution)/shard_map/ppermute | solution.py:21
  3.1 15.2 %collective-permute-start.8 = (bf16[128,640]{1,0:T(8,128)(2,1)}, bf16[128,640]{1,0:T(8,128)(2,1)S(1)}, u32[]{:S(2)}, u32[]{:S(2)}) collective-permute-start(bf16[128,640]{1,0:T(8,128)(2,1)} %refs_0_.1), channel_id=1, source_target_pairs={{0,2},{1,3},{2,0},{3,1},{4,6},{5,7},{6,4},{7,5},{8,10},{9,11},{10,... | collective-permute-start | bytes 491528 | tf_op jit(solution)/shard_map/ppermute | solution.py:21
  5.6 12.6 %collective-permute-start.9 = (bf16[128,640]{1,0:T(8,128)(2,1)}, bf16[128,640]{1,0:T(8,128)(2,1)S(1)}, u32[]{:S(2)}, u32[]{:S(2)}) collective-permute-start(bf16[128,640]{1,0:T(8,128)(2,1)} %refs_0_.1), channel_id=1, source_target_pairs={{0,3},{1,2},{2,1},{3,0},{4,7},{5,6},{6,5},{7,4},{8,11},{9,10},{10,... | collective-permute-start | bytes 491528 | tf_op jit(solution)/shard_map/ppermute | solution.py:21
  18.9 11.0 %collective-permute-start.10 = (bf16[64,2688]{1,0:T(8,128)(2,1)S(1)}, bf16[64,2688]{1,0:T(8,128)(2,1)S(1)}, u32[]{:S(2)}, u32[]{:S(2)}) collective-permute-start(bf16[64,2688]{1,0:T(8,128)(2,1)S(1)} %get-tuple-element.57.refs_0_), channel_id=1, source_target_pairs={{0,16},{4,20},{8,24},{12,28},{16,0},{20,4},{24,8},{28,12},{1,17},{... | collective-permute-start | bytes 1032200 | tf_op jit(solution)/shard_map/ppermute | solution.py:21
  20.5 10.8 %collective-permute-start.11 = (bf16[64,2688]{1,0:T(8,128)(2,1)S(1)}, bf16[64,2688]{1,0:T(8,128)(2,1)S(1)}, u32[]{:S(2)}, u32[]{:S(2)}) collective-permute-start(bf16[64,2688]{1,0:T(8,128)(2,1)S(1)} %get-tuple-element.58.refs_1_), channel_id=1, source_target_pairs={{0,8},{4,12},{8,0},{12,4},{16,24},{20,28},{24,16},{28,20},{1,9},{5... | collective-permute-start | bytes 1032200 | tf_op jit(solution)/shard_map/ppermute | solution.py:21
  22.0 13.0 %collective-permute-start.14 = (bf16[64,2688]{1,0:T(8,128)(2,1)S(1)}, bf16[64,2688]{1,0:T(8,128)(2,1)S(1)}, u32[]{:S(2)}, u32[]{:S(2)}) collective-permute-start(bf16[64,2688]{1,0:T(8,128)(2,1)S(1)} %get-tuple-element.57.refs_0_), channel_id=1, source_target_pairs={{0,8},{4,12},{8,0},{12,4},{16,24},{20,28},{24,16},{28,20},{1,9},{5... | collective-permute-start | bytes 1032200 | tf_op jit(solution)/shard_map/ppermute | solution.py:21
  22.5 12.5 %collective-permute-start.16 = (bf16[64,2688]{1,0:T(8,128)(2,1)S(1)}, bf16[64,2688]{1,0:T(8,128)(2,1)S(1)}, u32[]{:S(2)}, u32[]{:S(2)}) collective-permute-start(bf16[64,2688]{1,0:T(8,128)(2,1)S(1)} %get-tuple-element.58.refs_1_), channel_id=1, source_target_pairs={{0,16},{4,20},{8,24},{12,28},{16,0},{20,4},{24,8},{28,12},{1,17},{... | collective-permute-start | bytes 1032200 | tf_op jit(solution)/shard_map/ppermute | solution.py:21
  23.0 12.5 %collective-permute-start.20 = (bf16[64,2688]{1,0:T(8,128)(2,1)S(1)}, bf16[64,2688]{1,0:T(8,128)(2,1)S(1)}, u32[]{:S(2)}, u32[]{:S(2)}) collective-permute-start(bf16[64,2688]{1,0:T(8,128)(2,1)S(1)} %get-tuple-element.57.refs_0_), channel_id=1, source_target_pairs={{0,4},{4,0},{8,12},{12,8},{16,20},{20,16},{24,28},{28,24},{1,5},{5... | collective-permute-start | bytes 1032200 | tf_op jit(solution)/shard_map/ppermute | solution.py:21
  29.9 12.7 %collective-permute-start.21 = (bf16[64,2688]{1,0:T(8,128)(2,1)S(1)}, bf16[64,2688]{1,0:T(8,128)(2,1)S(1)}, u32[]{:S(2)}, u32[]{:S(2)}) collective-permute-start(bf16[64,2688]{1,0:T(8,128)(2,1)S(1)} %get-tuple-element.58.refs_1_), channel_id=1, source_target_pairs={{0,4},{4,0},{8,12},{12,8},{16,20},{20,16},{24,28},{28,24},{1,5},{5... | collective-permute-start | bytes 1032200 | tf_op jit(solution)/shard_map/ppermute | solution.py:21
  31.3 20.2 %collective-permute-start.12 = (bf16[64,2688]{1,0:T(8,128)(2,1)S(1)}, bf16[64,2688]{1,0:T(8,128)(2,1)S(1)}, u32[]{:S(2)}, u32[]{:S(2)}) collective-permute-start(bf16[64,2688]{1,0:T(8,128)(2,1)S(1)} %collective-permute-done.10.refs_0_), channel_id=1, source_target_pairs={{0,4},{4,0},{8,12},{12,8},{16,20},{20,16},{24,28},{28,24},{1,5},{5... | collective-permute-start | bytes 1032200 | tf_op jit(solution)/shard_map/ppermute | solution.py:21
  35.0 16.6 %collective-permute-start.13 = (bf16[64,2688]{1,0:T(8,128)(2,1)S(1)}, bf16[64,2688]{1,0:T(8,128)(2,1)S(1)}, u32[]{:S(2)}, u32[]{:S(2)}) collective-permute-start(bf16[64,2688]{1,0:T(8,128)(2,1)S(1)} %collective-permute-done.11.refs_1_), channel_id=1, source_target_pairs={{0,4},{4,0},{8,12},{12,8},{16,20},{20,16},{24,28},{28,24},{1,5},{5... | collective-permute-start | bytes 1032200 | tf_op jit(solution)/shard_map/ppermute | solution.py:21
  45.4 20.3 %collective-permute-start.18 = (bf16[64,2688]{1,0:T(8,128)(2,1)S(1)}, bf16[64,2688]{1,0:T(8,128)(2,1)S(1)}, u32[]{:S(2)}, u32[]{:S(2)}) collective-permute-start(bf16[64,2688]{1,0:T(8,128)(2,1)S(1)} %collective-permute-done.15.refs_0_), channel_id=1, source_target_pairs={{0,4},{4,0},{8,12},{12,8},{16,20},{20,16},{24,28},{28,24},{1,5},{5... | collective-permute-start | bytes 1032200 | tf_op jit(solution)/shard_map/ppermute | solution.py:21
  45.7 20.0 %collective-permute-start.19 = (bf16[64,2688]{1,0:T(8,128)(2,1)S(1)}, bf16[64,2688]{1,0:T(8,128)(2,1)S(1)}, u32[]{:S(2)}, u32[]{:S(2)}) collective-permute-start(bf16[64,2688]{1,0:T(8,128)(2,1)S(1)} %collective-permute-done.17.refs_1_), channel_id=1, source_target_pairs={{0,4},{4,0},{8,12},{12,8},{16,20},{20,16},{24,28},{28,24},{1,5},{5... | collective-permute-start | bytes 1032200 | tf_op jit(solution)/shard_map/ppermute | solution.py:21
  51.5 11.1 %collective-permute-start.2 = (bf16[320,384]{1,0:T(8,128)(2,1)S(1)}, bf16[320,384]{1,0:T(8,128)(2,1)S(1)}, u32[]{:S(2)}, u32[]{:S(2)}) collective-permute-start(bf16[320,384]{1,0:T(8,128)(2,1)S(1)} %copy-done.7), channel_id=1, source_target_pairs={{0,12},{4,8},{8,4},{12,0},{16,28},{20,24},{24,20},{28,16},{1,13},{... | collective-permute-start | bytes 737288 | tf_op jit(solution)/shard_map/ppermute | solution.py:21
  51.6 13.7 %collective-permute-start.3 = (bf16[320,384]{1,0:T(8,128)(2,1)S(1)}, bf16[320,384]{1,0:T(8,128)(2,1)S(1)}, u32[]{:S(2)}, u32[]{:S(2)}) collective-permute-start(bf16[320,384]{1,0:T(8,128)(2,1)S(1)} %copy-done.6), channel_id=1, source_target_pairs={{0,16},{4,20},{8,24},{12,28},{16,0},{20,4},{24,8},{28,12},{1,17},{... | collective-permute-start | bytes 737288 | tf_op jit(solution)/shard_map/ppermute | solution.py:21
  58.8 11.3 %collective-permute-start.4 = (bf16[320,384]{1,0:T(8,128)(2,1)S(1)}, bf16[320,384]{1,0:T(8,128)(2,1)S(1)}, u32[]{:S(2)}, u32[]{:S(2)}) collective-permute-start(bf16[320,384]{1,0:T(8,128)(2,1)S(1)} %copy-done.5), channel_id=1, source_target_pairs={{0,20},{4,16},{8,28},{12,24},{16,4},{20,0},{24,12},{28,8},{1,21},{... | collective-permute-start | bytes 737288 | tf_op jit(solution)/shard_map/ppermute | solution.py:21
  65.3 12.1 %collective-permute-start.6 = (bf16[320,384]{1,0:T(8,128)(2,1)S(1)}, bf16[320,384]{1,0:T(8,128)(2,1)S(1)}, u32[]{:S(2)}, u32[]{:S(2)}) collective-permute-start(bf16[320,384]{1,0:T(8,128)(2,1)S(1)} %get-tuple-element.101), channel_id=1, source_target_pairs={{0,28},{4,24},{8,20},{12,16},{16,12},{20,8},{24,4},{28,0},{1,29},{... | collective-permute-start | bytes 737288 | tf_op jit(solution)/shard_map/ppermute | solution.py:21
  65.7 18.9 %collective-permute-start.22 = (bf16[64,2688]{1,0:T(8,128)(2,1)S(1)}, bf16[64,2688]{1,0:T(8,128)(2,1)S(1)}, u32[]{:S(2)}, u32[]{:S(2)}) collective-permute-start(bf16[64,2688]{1,0:T(8,128)(2,1)S(1)} %collective-permute-done.14.refs_0_), channel_id=1, source_target_pairs={{0,4},{4,0},{8,12},{12,8},{16,20},{20,16},{24,28},{28,24},{1,5},{5... | collective-permute-start | bytes 1032200 | tf_op jit(solution)/shard_map/ppermute | solution.py:21
  65.7 18.9 %collective-permute-start.23 = (bf16[64,2688]{1,0:T(8,128)(2,1)S(1)}, bf16[64,2688]{1,0:T(8,128)(2,1)S(1)}, u32[]{:S(2)}, u32[]{:S(2)}) collective-permute-start(bf16[64,2688]{1,0:T(8,128)(2,1)S(1)} %collective-permute-done.16.refs_1_), channel_id=1, source_target_pairs={{0,4},{4,0},{8,12},{12,8},{16,20},{20,16},{24,28},{28,24},{1,5},{5... | collective-permute-start | bytes 1032200 | tf_op jit(solution)/shard_map/ppermute | solution.py:21
  84.4 14.2 %collective-permute-start.33 = (bf16[256,1280]{1,0:T(8,128)(2,1)S(1)}, bf16[256,1280]{1,0:T(8,128)(2,1)S(1)}, u32[]{:S(2)}, u32[]{:S(2)}) collective-permute-start(bf16[256,1280]{1,0:T(8,128)(2,1)S(1)} %get-tuple-element.91), channel_id=1, source_target_pairs={{0,4},{4,0},{8,12},{12,8},{16,20},{20,16},{24,28},{28,24},{1,5},{5... | collective-permute-start | bytes 1966088 | tf_op jit(solution)/shard_map/ppermute | solution.py:21
  101.9 14.6 %collective-permute-start.26 = (bf16[128,1280]{1,0:T(8,128)(2,1)S(1)}, bf16[128,1280]{1,0:T(8,128)(2,1)S(1)}, u32[]{:S(2)}, u32[]{:S(2)}) collective-permute-start(bf16[128,1280]{1,0:T(8,128)(2,1)S(1)} %pad_maximum_fusion.2), channel_id=1, source_target_pairs={{0,16},{4,20},{8,24},{12,28},{16,0},{20,4},{24,8},{28,12},{1,17},{... | collective-permute-start | bytes 983048 | tf_op jit(solution)/shard_map/ppermute | solution.py:21
  102.7 15.0 %collective-permute-start.27 = (bf16[128,1280]{1,0:T(8,128)(2,1)S(1)}, bf16[128,1280]{1,0:T(8,128)(2,1)S(1)}, u32[]{:S(2)}, u32[]{:S(2)}) collective-permute-start(bf16[128,1280]{1,0:T(8,128)(2,1)S(1)} %pad_maximum_fusion.3), channel_id=1, source_target_pairs={{0,8},{4,12},{8,0},{12,4},{16,24},{20,28},{24,16},{28,20},{1,9},{5... | collective-permute-start | bytes 983048 | tf_op jit(solution)/shard_map/ppermute | solution.py:21
  125.7 15.5 %collective-permute-start.31 = (bf16[128,640]{1,0:T(8,128)(2,1)S(1)}, bf16[128,640]{1,0:T(8,128)(2,1)S(1)}, u32[]{:S(2)}, u32[]{:S(2)}) collective-permute-start(bf16[128,640]{1,0:T(8,128)(2,1)S(1)} %get-tuple-element.126), channel_id=1, source_target_pairs={{0,2},{1,3},{2,0},{3,1},{4,6},{5,7},{6,4},{7,5},{8,10},{9,11},{10,... | collective-permute-start | bytes 491528 | tf_op jit(solution)/shard_map/ppermute | solution.py:21
  130.2 11.0 %collective-permute-start.30 = (bf16[128,640]{1,0:T(8,128)(2,1)S(1)}, bf16[128,640]{1,0:T(8,128)(2,1)S(1)}, u32[]{:S(2)}, u32[]{:S(2)}) collective-permute-start(bf16[128,640]{1,0:T(8,128)(2,1)S(1)} %get-tuple-element.125), channel_id=1, source_target_pairs={{0,3},{1,2},{2,1},{3,0},{4,7},{5,6},{6,5},{7,4},{8,11},{9,10},{10,... | collective-permute-start | bytes 491528 | tf_op jit(solution)/shard_map/ppermute | solution.py:21
  (25 other events, 233.8 us)
